TPU v7x, 256 devices: a whole 4x4x8 slice. The times are simulated.
256 devices in a mesh: samp: 64 (over y, z, core), gene: 4 (over x).
Axes of the slice: x: 4, y: 4, z: 8, core: 2. Of those that a mesh axis runs over, the one named last changes fastest.
Arguments:
- genotypes: int32 [2048, 32768], P('samp', 'gene'), may hold values from -2147483648 to 1789569706, as said below
- allele_freq: float32 [32768], P('gene'), may hold values from 0.035 to 0.56
- sample_weight: float32 [16, 2048], P(None, 'samp'), may hold values from 0.2 to 2
- residual: float32 [16, 2048], P(None, 'samp'), may hold values from -12 to 12
- variant_weight: float32 [32768], P('gene'), may hold values from 0.2 to 4
- block_gene: int32 [256], replicated, may hold values from 0 to 127, as said below
- gene_variants: int32 [128], replicated, may hold values from 1 to 384, as said below
Outputs:
- burden_z: float32 [128], replicated
- skat_z: float32 [128], replicated
Inputs may be any that keep to these rules, and one draw needn't show every extreme that they name: Each word holds 16 dosages 0, 1 or 2: bits 2k and 2k+1 of genotypes[i, v] are the dosage of variant slot v in sample (k, i); a dosage 2 in the top field sets the sign bit. `block_gene`: never falling; the blocks come in aligned groups of four, each shared by two consecutive genes, so every gene has 1 to 3 blocks. `gene_variants`: A gene with m blocks has from (m - 1) * 128 + 1 to m * 128 live variants; the slots after them in its last block are padding.
All inputs are finite; a program needn't handle non-finite values.
Results may differ from a plain program's by a relative error of at most 0.0037.
Values sent between devices are 32-bit elements; how exact they have to be, the bound alone decides.
A program may use at most 64 MiB of HBM per device.

v0:
```python
import jax
import jax.numpy as jnp
from jax import lax
from jax.sharding import Mesh
from jax.sharding import PartitionSpec as P

BLK = 128
SAMP = ("samp_0", "samp_1", "samp_2")
SAMP_GENE = ("samp_0", "samp_1", "samp_2", "gene")


def turned_gather(arrays, axis, dims):
    turned = [jnp.moveaxis(a, dim, 0) for a, dim in zip(arrays, dims)]
    both = jnp.concatenate([t.reshape(len(t), -1) for t in turned], axis=1)
    result, at, done = (lax.all_gather(both, axis, axis=0, tiled=True), 0, [])
    for t, dim in zip(turned, dims):
        share = result[:, at : at + t[0].size].reshape(-1, *t.shape[1:])
        done.append(jnp.moveaxis(share, 0, dim))
        at += t[0].size
    return tuple(done)


def by_axis(array, axes):
    for axis in axes:
        array = lax.psum(array, axis)
    return array


def unpack(packed_words, allele_part, root_weight):
    fields = root_weight.shape[0]
    offsets = 2 * jnp.arange(fields, dtype=jnp.int32)
    dosage = jnp.bitwise_and(jnp.right_shift(packed_words[None, :, :], offsets[:, None, None]), 3)
    centered = dosage.astype(jnp.float32) - 2.0 * allele_part[None, None, :]
    return (root_weight[:, :, None] * centered).astype(jnp.bfloat16)


def block_grams(scaled, block_count):
    stacked = scaled.reshape(scaled.shape[0] * scaled.shape[1], block_count, BLK)
    return jnp.einsum("sbu,sbv->buv", stacked, stacked, preferred_element_type=jnp.float32)


def block_stats(gram_part, scores, effective):
    weighted_score = effective * scores
    burden_sum = jnp.sum(weighted_score, axis=1)
    skat_sum = jnp.sum(weighted_score * weighted_score, axis=1)
    image = jnp.einsum("buv,bv->bu", gram_part, effective)
    burden_var = jnp.sum(effective * image, axis=1)
    diagonal = jnp.diagonal(gram_part, axis1=1, axis2=2)
    trace_one = jnp.sum(effective * effective * diagonal, axis=1)
    scaled_gram = effective[:, :, None] * gram_part * effective[:, None, :]
    trace_two = jnp.sum(scaled_gram * scaled_gram, axis=(1, 2))
    return jnp.stack([burden_sum, burden_var, skat_sum, trace_one, trace_two])


def live_weights(block_ids, variant_part, block_gene, gene_variants):
    total_blocks = block_gene.shape[0]
    genes = gene_variants.shape[0]
    chosen = block_ids[:, None] == jnp.arange(total_blocks, dtype=jnp.int32)[None, :]
    gene_of = jnp.sum(jnp.where(chosen, block_gene[None, :], 0), axis=1)
    first_block = jnp.sum((block_gene[None, :] < gene_of[:, None]).astype(jnp.int32), axis=1)
    member = gene_of[:, None] == jnp.arange(genes, dtype=jnp.int32)[None, :]
    counted = jnp.sum(jnp.where(member, gene_variants[None, :], 0), axis=1)
    column = jnp.arange(BLK, dtype=jnp.int32)
    is_live = (block_ids - first_block)[:, None] * BLK + column[None, :] < counted[:, None]
    return (variant_part * is_live.astype(jnp.float32), member.astype(jnp.float32))


def local(
    genotypes, allele_freq, sample_weight, residual, variant_weight, block_gene, gene_variants
):
    local_blocks = genotypes.shape[1] // BLK
    owned_count = local_blocks // lax.axis_size(SAMP)
    samp_index = lax.axis_index(SAMP)
    gene_index = lax.axis_index("gene")
    block_ids = (
        gene_index * local_blocks
        + samp_index * owned_count
        + jnp.arange(owned_count, dtype=jnp.int32)
    )
    variant_blocks = variant_weight.reshape(local_blocks, BLK)
    own_weights = lax.dynamic_slice_in_dim(variant_blocks, samp_index * owned_count, owned_count, 0)
    effective, member = live_weights(block_ids, own_weights, block_gene, gene_variants)
    own_words = lax.all_to_all(genotypes, SAMP, split_axis=1, concat_axis=0, tiled=True)
    all_weight, all_residual = turned_gather((sample_weight, residual), SAMP, (1, 1))
    own_freq = lax.dynamic_slice_in_dim(
        allele_freq, samp_index * owned_count * BLK, owned_count * BLK, 0
    )
    root_all = jnp.sqrt(all_weight)
    weighted_residual = (root_all * all_residual).astype(jnp.bfloat16)
    scaled = unpack(own_words, own_freq, root_all)
    gram_part = block_grams(scaled, owned_count)
    flattened = scaled.reshape(scaled.shape[0] * scaled.shape[1], owned_count * BLK)
    scores = jnp.dot(
        weighted_residual.reshape(1, -1), flattened, preferred_element_type=jnp.float32
    )
    variance = jnp.sum(all_weight * all_residual * all_residual) / (
        all_weight.shape[0] * all_weight.shape[1]
    )
    gene_parts = jnp.dot(block_stats(gram_part, scores, effective), member)
    totals = by_axis(gene_parts, SAMP_GENE)
    burden = totals[0] / jnp.sqrt(variance * totals[1])
    skat_score = (totals[2] - variance * totals[3]) / (variance * jnp.sqrt(2.0 * totals[4]))
    return (burden, skat_score)


def solution(mesh):
    torus = Mesh(
        mesh.devices.reshape(4, 8, 2, mesh.shape["gene"]), ("samp_0", "samp_1", "samp_2", "gene")
    )
    placed = (P(SAMP, "gene"), P("gene"), P(None, SAMP), P(None, SAMP), P("gene"), P(), P())
    return jax.shard_map(local, mesh=torus, in_specs=placed, out_specs=(P(), P()), check_vma=False)
```

profile of v0, /device:TPU:8, one launch (start us, length us, event | category | flops | bytes accessed | tf_op | source)
XLA Modules:
  0.0 156.2 jit_solution(2203239968844073498)
XLA Ops:
  0.6 0.0 copy-start
  0.7 1.2 copy-done
  1.9 1.1 copy_bitcast_fusion
  3.0 12.1 %all-to-all-start = ((s32[32,64,128]{2,0,1:T(8,128)}), s32[32,64,128]{2,0,1:T(8,128)S(1)}, u32[]{:S(2)}, u32[]{:S(2)}) async-start(s32[32,64,128]{2,0,1:T(8,128)} %copy_bitcast_fusion), calls=%async_computation | async-start | bytes 2097152 | tf_op jit(solution)/shard_map/all_to_all | solution.py:83
  15.1 1.3 fusion.19
  16.4 2.0 %fusion.20 = s32[]{:T(128)} fusion(s32[256]{0:T(256)} %param.12, s32[]{:T(128)} %fusion.19), kind=kLoop, calls=%fused_computation.36 | loop fusion | flops 767 | bytes 1032 | tf_op jit(solution)/shard_map/reduce_sum | solution.py:60
  19.1 0.8 copy.15
  19.8 0.8 copy.16
  20.6 0.1 pad_maximum_fusion
  20.7 62.9 %all_gather.3 = f32[2048,32]{1,0:T(8,128)S(1)} all-gather(f32[32,32]{1,0:T(8,128)S(1)} %pad_maximum_fusion), channel_id=1, replica_groups=mesh['samp_0'=4,'samp_1'=8,'samp_2'=2,'gene'=4] {'samp_0','samp_1','samp..., dimensions={0}, use_global_device_ids=true | all-gather | bytes 266240 | tf_op jit(solution)/shard_map/all_gather | solution.py:15
  83.6 1.9 %fusion.15 = (f32[]{:T(128)}, bf16[16,2048,1]{0,1,2:T(8,128)(2,1)}, f32[16,2048]{0,1:T(8,128)S(1)}) fusion(f32[2048,32]{1,0:T(8,128)S(1)} %all_gather.3), kind=kLoop, calls=%fused_computation.19 | loop fusion | flops 163839 | bytes 458756 | tf_op jit(solution)/shard_map/reduce_sum | solution.py:96
  85.5 1.4 copy.21
  86.9 0.3 copy.17
  87.8 0.7 fusion.22
  88.5 0.8 dynamic-slice_multiply_fusion
  89.3 1.3 fusion.21
  90.6 0.0 all-to-all-done
  90.6 0.3 copy.19
  90.9 6.6 %multiply_convert_fusion.14 = bf16[16,2048,128]{1,2,0:T(8,128)(2,1)} fusion(f32[128]{0:T(128)S(1)} %dynamic-slice_multiply_fusion, s32[16]{0:T(128)S(1)} %iota_multiply_fusion, s32[2048,128]{0,1:T(8,128)S(1)} %copy.19, f32[16,2048]{1,0:T(8,128)S(1)} %copy.17), kind=kLoop, calls=%fused_computation.1.clone.clone.clone.clone.2 | loop fusion | flops 25165824 | bytes 9568832 | tf_op jit(solution)/shard_map/sbu,sbv->buv/dot_general | solution.py:39
  97.5 8.1 %fusion.12 = f32[128,128]{1,0:T(8,128)S(1)} fusion(bf16[16,2048,128]{1,2,0:T(8,128)(2,1)} %multiply_convert_fusion.14), kind=kOutput, calls=%fused_computation.15 | convolution fusion | flops 1073741824 | bytes 8454144 | tf_op jit(solution)/shard_map/sbu,sbv->buv/dot_general | solution.py:39
  105.6 1.4 gather_fusion
  107.0 1.9 %fusion.23 = (f32[]{:T(128)}, f32[1,128]{1,0:T(1,128)S(1)}) fusion(f32[128]{0:T(128)S(1)} %gather_fusion, f32[64,128]{1,0:T(8,128)} %bitcast.70, s32[]{:T(128)S(6)} %select_n.22, s32[]{:T(128)} %fusion.21, s32[]{:T(128)S(6)} %mul.117), kind=kLoop, calls=%fused_computation.40 | loop fusion | flops 767 | bytes 1552 | tf_op jit(solution)/shard_map/reduce_sum | solution.py:49
  109.0 0.7 fusion.17
  109.7 3.9 %multiply_reduce_fusion.1 = (f32[]{:T(128)}, f32[]{:T(128)}) fusion(f32[1,128]{1,0:T(1,128)S(1)} %get-tuple-element.5, bf16[16,2048,1]{1,2,0:T(2,128)(2,1)S(1)} %copy.21, f32[128]{0:T(128)S(1)} %dynamic-slice_multiply_fusion, s32[16]{0:T(128)S(1)} %iota_multiply_fusion, s32[2048,128]{0,1:T(8,128)S(1)} %copy.19, f32[16,2048]{1,0:T(8,128)S(1)} %copy.17), kind=kOutput, calls=%fused_computation.45 | convolution fusion | flops 33554944 | bytes 1246280 | tf_op jit(solution)/shard_map/dot_general | solution.py:93
  113.6 0.7 multiply_reduce_fusion
  114.3 3.3 %stack.23 = f32[5,1]{0,1:T(1,128)S(1)} concatenate(f32[1,1]{0,1:T(1,128)} %bitcast.10, f32[1,1]{0,1:T(1,128)} %bitcast.15, f32[1,1]{0,1:T(1,128)} %bitcast.16, f32[1,1]{0,1:T(1,128)} %bitcast.19, f32[1,1]{0,1:T(1,128)} %bitcast.20), dimensions={0} | concatenate | bytes 40 | tf_op jit(solution)/shard_map/stack | solution.py:52
  117.6 0.1 broadcast_multiply_fusion
  117.7 8.6 %psum.28 = f32[5,128]{1,0:T(8,128)S(1)} all-reduce(f32[5,128]{1,0:T(8,128)S(1)} %broadcast_multiply_fusion), channel_id=1, replica_groups=mesh['samp_0'=4,'samp_1'=8,'samp_2'=2,'gene'=4] {'samp_0'}, use_global_device_ids=true, to_apply=%region_8.9 | all-reduce | flops 640 | bytes 5120 | tf_op jit(solution)/shard_map/psum | solution.py:25
  126.2 16.5 %psum.29 = f32[5,128]{1,0:T(8,128)S(1)} all-reduce(f32[5,128]{1,0:T(8,128)S(1)} %psum.28), channel_id=1, replica_groups=mesh['samp_0'=4,'samp_1'=8,'samp_2'=2,'gene'=4] {'samp_1'}, use_global_device_ids=true, to_apply=%region_9.10 | all-reduce | flops 640 | bytes 5120 | tf_op jit(solution)/shard_map/psum | solution.py:25
  142.8 2.5 %psum.30 = f32[5,128]{1,0:T(8,128)S(1)} all-reduce(f32[5,128]{1,0:T(8,128)S(1)} %psum.29), channel_id=1, replica_groups=mesh['samp_0'=4,'samp_1'=8,'samp_2'=2,'gene'=4] {'samp_2'}, use_global_device_ids=true, to_apply=%region_10.11 | all-reduce | flops 640 | bytes 5120 | tf_op jit(solution)/shard_map/psum | solution.py:25
  145.2 10.5 %psum.31 = f32[5,128]{1,0:T(8,128)S(1)} all-reduce(f32[5,128]{1,0:T(8,128)S(1)} %psum.30), channel_id=1, replica_groups=mesh['samp_0'=4,'samp_1'=8,'samp_2'=2,'gene'=4] {'gene'}, use_global_device_ids=true, to_apply=%region_11.12 | all-reduce | flops 640 | bytes 5120 | tf_op jit(solution)/shard_map/psum | solution.py:25
  155.7 0.5 fusion.25
  (4 shorter events, 0.0 us)
Async XLA Ops:
  0.6 1.2 copy-start
  0.6 88.6 %copy-start.1 = (s32[128]{0:T(128)S(1)}, s32[128]{0:T(128)}, u32[]{:S(2)}) copy-start(s32[128]{0:T(128)} %param.13) | copy-start | bytes 1540
  3.0 87.6 %all-to-all-start = ((s32[32,64,128]{2,0,1:T(8,128)}), s32[32,64,128]{2,0,1:T(8,128)S(1)}, u32[]{:S(2)}, u32[]{:S(2)}) async-start(s32[32,64,128]{2,0,1:T(8,128)} %copy_bitcast_fusion), calls=%async_computation | async-start | bytes 2097152 | tf_op jit(solution)/shard_map/all_to_all | solution.py:83
where the time goes:
time: 157 us; the launch traced here: 156 us
  blocking collectives  101 us (64%)
  other arithmetic  17.8 us (11%)
  matrix products  12.7 us (8%)
  starting transfers between devices  12.1 us (8%)
  local copies, waits for them, and re-layouts  10.6 us (7%)
  between operations  2.05 us (1%)
    all_gather x1, blocking collectives, turned_gather(): result, at, done = (lax.all_gather(both, axis, axis=0, tiled=True), 0, [])  62.9 us
    psum x4, blocking collectives, by_axis(): array = lax.psum(array, axis)  38 us
    all_to_all x1, starting transfers between devices, local(): lax.all_to_all(genotypes, SAMP, split_axis=1, concat_axis=0, tiled=True)  12.1 us
    dot_general x1, matrix products, block_grams(): jnp.einsum('sbu,sbv->buv', stacked, stacked, preferred_element_type=jnp.f...  8.1 us
    dot_general x1, other arithmetic, block_grams(): jnp.einsum('sbu,sbv->buv', stacked, stacked, preferred_element_type=jnp.f...  6.58 us
    dot_general x1, matrix products, local(): jnp.dot(weighted_residual.reshape(1, -1), flattened, preferred_element_ty...  3.91 us
    another operation x1, local copies, waits for them, and re-layouts, block_stats(): return jnp.stack([burden_sum, burden_var, skat_sum, trace_one, trace_two])  3.27 us
  transfers between devices with their start and end apart: 1, of which 0 were waited for; matrix products, arithmetic and copies ran while one was open for 7% of the time, Pallas kernels for 0%

commit v1 on v0

--- a/solution.py
+++ b/solution.py
@@ -7,6 +7,12 @@
 BLK = 128
 SAMP = ("samp_0", "samp_1", "samp_2")
 SAMP_GENE = ("samp_0", "samp_1", "samp_2", "gene")
+
+
+def add_all(value, mesh_axis):
+    pieces = lax.all_gather(value, mesh_axis, axis=0, tiled=False)
+    total = pieces.sum(axis=0)
+    return total
 
 
 def turned_gather(arrays, axis, dims):
@@ -22,7 +28,7 @@
 
 def by_axis(array, axes):
     for axis in axes:
-        array = lax.psum(array, axis)
+        array = add_all(array, axis)
     return array
 
 

time: 157 us -> 171 us (1.089)
  blocking collectives: 101 us -> 114 us
    all_gather x0 -> x4, blocking collectives: none -> 50.9 us  [add_all(): pieces = lax.all_gather(value, mesh_axis, axis=0, tiled=False)]
    psum x4 -> x0, blocking collectives: 38 us -> none  [by_axis(): array = lax.psum(array, axis)]
where the time goes in v1:
time: 171 us; the launch traced here: 169 us
  blocking collectives  114 us (67%)
  other arithmetic  17.8 us (10%)
  matrix products  12.7 us (7%)
  starting transfers between devices  12.1 us (7%)
  local copies, waits for them, and re-layouts  10.6 us (6%)
  between operations  2.05 us (1%)
    all_gather x1, blocking collectives, turned_gather(): result, at, done = (lax.all_gather(both, axis, axis=0, tiled=True), 0, [])  62.9 us
    all_gather x4, blocking collectives, add_all(): pieces = lax.all_gather(value, mesh_axis, axis=0, tiled=False)  50.9 us
    all_to_all x1, starting transfers between devices, local(): lax.all_to_all(genotypes, SAMP, split_axis=1, concat_axis=0, tiled=True)  12.1 us
    dot_general x1, matrix products, block_grams(): jnp.einsum('sbu,sbv->buv', stacked, stacked, preferred_element_type=jnp.f...  8.1 us
    dot_general x1, other arithmetic, block_grams(): jnp.einsum('sbu,sbv->buv', stacked, stacked, preferred_element_type=jnp.f...  6.58 us
    dot_general x1, matrix products, local(): jnp.dot(weighted_residual.reshape(1, -1), flattened, preferred_element_ty...  3.91 us
  transfers between devices with their start and end apart: 1, of which 0 were waited for; matrix products, arithmetic and copies ran while one was open for 7% of the time, Pallas kernels for 0%

profile of v1, /device:TPU:8, one launch (start us, length us, event | category | flops | bytes accessed | tf_op | source)
XLA Modules:
  0.0 169.1 jit_solution(11221003486202392358)
XLA Ops:
  0.6 0.0 copy-start
  0.7 1.2 copy-done
  1.9 1.1 copy_bitcast_fusion
  3.0 12.1 %all-to-all-start = ((s32[32,64,128]{2,0,1:T(8,128)}), s32[32,64,128]{2,0,1:T(8,128)S(1)}, u32[]{:S(2)}, u32[]{:S(2)}) async-start(s32[32,64,128]{2,0,1:T(8,128)} %copy_bitcast_fusion), calls=%async_computation | async-start | bytes 2097152 | tf_op jit(solution)/shard_map/all_to_all | solution.py:89
  15.1 1.3 fusion.19
  16.4 2.0 %fusion.20 = s32[]{:T(128)} fusion(s32[256]{0:T(256)} %param.12, s32[]{:T(128)} %fusion.19), kind=kLoop, calls=%fused_computation.36 | loop fusion | flops 767 | bytes 1032 | tf_op jit(solution)/shard_map/reduce_sum | solution.py:66
  19.1 0.8 copy.15
  19.8 0.8 copy.16
  20.6 0.1 pad_maximum_fusion
  20.7 62.9 %all_gather.27 = f32[2048,32]{1,0:T(8,128)S(1)} all-gather(f32[32,32]{1,0:T(8,128)S(1)} %pad_maximum_fusion), channel_id=1, replica_groups=mesh['samp_0'=4,'samp_1'=8,'samp_2'=2,'gene'=4] {'samp_0','samp_1','samp..., dimensions={0}, use_global_device_ids=true | all-gather | bytes 266240 | tf_op jit(solution)/shard_map/all_gather | solution.py:21
  83.6 1.9 %fusion.15 = (f32[]{:T(128)}, bf16[16,2048,1]{0,1,2:T(8,128)(2,1)}, f32[16,2048]{0,1:T(8,128)S(1)}) fusion(f32[2048,32]{1,0:T(8,128)S(1)} %all_gather.27), kind=kLoop, calls=%fused_computation.19 | loop fusion | flops 163839 | bytes 458756 | tf_op jit(solution)/shard_map/reduce_sum | solution.py:102
  85.5 1.4 copy.21
  86.9 0.3 copy.17
  87.8 0.7 fusion.22
  88.5 0.8 dynamic-slice_multiply_fusion
  89.3 1.3 fusion.21
  90.6 0.0 all-to-all-done
  90.6 0.3 copy.19
  90.9 6.6 %multiply_convert_fusion.14 = bf16[16,2048,128]{1,2,0:T(8,128)(2,1)} fusion(f32[128]{0:T(128)S(1)} %dynamic-slice_multiply_fusion, s32[16]{0:T(128)S(1)} %iota_multiply_fusion, s32[2048,128]{0,1:T(8,128)S(1)} %copy.19, f32[16,2048]{1,0:T(8,128)S(1)} %copy.17), kind=kLoop, calls=%fused_computation.1.clone.clone.clone.clone.2 | loop fusion | flops 25165824 | bytes 9568832 | tf_op jit(solution)/shard_map/sbu,sbv->buv/dot_general | solution.py:45
  97.5 8.1 %fusion.12 = f32[128,128]{1,0:T(8,128)S(1)} fusion(bf16[16,2048,128]{1,2,0:T(8,128)(2,1)} %multiply_convert_fusion.14), kind=kOutput, calls=%fused_computation.15 | convolution fusion | flops 1073741824 | bytes 8454144 | tf_op jit(solution)/shard_map/sbu,sbv->buv/dot_general | solution.py:45
  105.6 1.4 gather_fusion
  107.0 1.9 %fusion.23 = (f32[]{:T(128)}, f32[1,128]{1,0:T(1,128)S(1)}) fusion(f32[128]{0:T(128)S(1)} %gather_fusion, f32[64,128]{1,0:T(8,128)} %bitcast.78, s32[]{:T(128)S(6)} %select_n.22, s32[]{:T(128)} %fusion.21, s32[]{:T(128)S(6)} %mul.117), kind=kLoop, calls=%fused_computation.40 | loop fusion | flops 767 | bytes 1552 | tf_op jit(solution)/shard_map/reduce_sum | solution.py:55
  109.0 0.7 fusion.17
  109.7 3.9 %multiply_reduce_fusion.1 = (f32[]{:T(128)}, f32[]{:T(128)}) fusion(f32[1,128]{1,0:T(1,128)S(1)} %get-tuple-element.5, bf16[16,2048,1]{1,2,0:T(2,128)(2,1)S(1)} %copy.21, f32[128]{0:T(128)S(1)} %dynamic-slice_multiply_fusion, s32[16]{0:T(128)S(1)} %iota_multiply_fusion, s32[2048,128]{0,1:T(8,128)S(1)} %copy.19, f32[16,2048]{1,0:T(8,128)S(1)} %copy.17), kind=kOutput, calls=%fused_computation.45 | convolution fusion | flops 33554944 | bytes 1246280 | tf_op jit(solution)/shard_map/dot_general | solution.py:99
  113.6 0.7 multiply_reduce_fusion
  114.3 3.3 %stack.23 = f32[5,1]{0,1:T(1,128)S(1)} concatenate(f32[1,1]{0,1:T(1,128)} %bitcast.10, f32[1,1]{0,1:T(1,128)} %bitcast.15, f32[1,1]{0,1:T(1,128)} %bitcast.16, f32[1,1]{0,1:T(1,128)} %bitcast.19, f32[1,1]{0,1:T(1,128)} %bitcast.20), dimensions={0} | concatenate | bytes 40 | tf_op jit(solution)/shard_map/stack | solution.py:58
  117.6 0.1 multiply_bitcast_fusion
  117.7 12.0 %all-gather.4 = f32[4,5,128]{2,1,0:T(8,128)S(1)} all-gather(f32[1,5,128]{2,1,0:T(8,128)S(1)} %multiply_bitcast_fusion), channel_id=2, replica_groups=mesh['samp_0'=4,'samp_1'=8,'samp_2'=2,'gene'=4] {'samp_0'}, dimensions={0}, use_global_device_ids=true | all-gather | bytes 12800 | tf_op jit(solution)/shard_map/all_gather | solution.py:13
  129.7 24.7 %all-gather.5 = f32[8,5,128]{2,1,0:T(8,128)S(1)} all-gather(f32[1,5,128]{2,1,0:T(8,128)S(1)} %bitcast.75), channel_id=3, replica_groups=mesh['samp_0'=4,'samp_1'=8,'samp_2'=2,'gene'=4] {'samp_1'}, dimensions={0}, use_global_device_ids=true | all-gather | bytes 23040 | tf_op jit(solution)/shard_map/all_gather | solution.py:13
  154.4 1.8 %all-gather.6 = f32[2,5,128]{2,1,0:T(8,128)S(1)} all-gather(f32[1,5,128]{2,1,0:T(8,128)S(1)} %bitcast.73), channel_id=4, replica_groups=mesh['samp_0'=4,'samp_1'=8,'samp_2'=2,'gene'=4] {'samp_2'}, dimensions={0}, use_global_device_ids=true | all-gather | bytes 7680 | tf_op jit(solution)/shard_map/all_gather | solution.py:13
  156.2 12.4 %all-gather.7 = f32[4,5,128]{2,1,0:T(8,128)S(1)} all-gather(f32[1,5,128]{2,1,0:T(8,128)S(1)} %bitcast.74), channel_id=5, replica_groups=mesh['samp_0'=4,'samp_1'=8,'samp_2'=2,'gene'=4] {'gene'}, dimensions={0}, use_global_device_ids=true | all-gather | bytes 12800 | tf_op jit(solution)/shard_map/all_gather | solution.py:13
  168.6 0.5 fusion.25
  (8 shorter events, 0.1 us)
Async XLA Ops:
  0.6 1.2 copy-start
  0.6 88.6 %copy-start.1 = (s32[128]{0:T(128)S(1)}, s32[128]{0:T(128)}, u32[]{:S(2)}) copy-start(s32[128]{0:T(128)} %param.13) | copy-start | bytes 1540
  3.0 87.6 %all-to-all-start = ((s32[32,64,128]{2,0,1:T(8,128)}), s32[32,64,128]{2,0,1:T(8,128)S(1)}, u32[]{:S(2)}, u32[]{:S(2)}) async-start(s32[32,64,128]{2,0,1:T(8,128)} %copy_bitcast_fusion), calls=%async_computation | async-start | bytes 2097152 | tf_op jit(solution)/shard_map/all_to_all | solution.py:89
